TPU v7x, 32 devices: a whole 2x2x4 slice. The times are simulated.
32 devices in a mesh: row: 16 (over z, x, core), col: 2 (over y).
Axes of the slice: x: 2, y: 2, z: 4, core: 2. Of those that a mesh axis runs over, the one named last changes fastest.
Arguments:
- occupied_waves: bfloat16 [1024, 32768], P('row', 'col'), may hold values from -6 to 6
- virtual_waves: bfloat16 [512, 32768], P('row', 'col'), may hold values from -6 to 6
- occupied_decay: float32 [1024], replicated, may hold values from 0.02 to 1
- virtual_decay: float32 [512], replicated, may hold values from 0.02 to 1
Outputs:
- spectrum_real: float32 [512, 32, 1024], P('row', 'col')
- spectrum_imaginary: float32 [512, 32, 1024], P('row', 'col')
All inputs are finite; a program needn't handle non-finite values.
Results may differ from a plain program's by a relative error of at most 0.0041.
Values may be sent and summed in bfloat16 or wider, within the bound.
A program may use at most 128 MiB of HBM per device.

v0:
```python
import math
import jax
import jax.numpy as jnp
from jax import lax
from jax.sharding import PartitionSpec as P

NOCC = 1024
NVIR = 512
NA = 32
NB = 32
NC = 32
ROWS_DEV = 32
NGRID = 32768


def tables(length):
    index = jnp.arange(length, dtype=jnp.int32)
    phase = index[:, None] * index[None, :] % length
    angle = phase.astype(jnp.float32) * (2.0 * math.pi / length)
    return (jnp.cos(angle), jnp.sin(angle))


def apply_table(form, data, table):
    return jnp.einsum(form, data, table, precision=lax.Precision.HIGHEST)


def real_step(data, form, length):
    cosine, sine = tables(length)
    return (apply_table(form, data, cosine), -apply_table(form, data, sine))


def complex_step(real_part, imag_part, form, length):
    cosine, sine = tables(length)
    new_real = apply_table(form, real_part, cosine) + apply_table(form, imag_part, sine)
    new_imag = apply_table(form, imag_part, cosine) - apply_table(form, real_part, sine)
    return (new_real, new_imag)


def scale_rows(waves, decay):
    return (waves * decay[:, None]).astype(jnp.bfloat16)


def place(waves, window, start_col):
    block_cols = waves.shape[1]
    buffer = jnp.zeros((waves.shape[0], window + block_cols), jnp.bfloat16)
    buffer = lax.dynamic_update_slice(buffer, waves, (jnp.int32(0), start_col))
    return buffer[:, :window]


def on_device(occupied_waves, virtual_waves, occupied_decay, virtual_decay):
    block_cols = occupied_waves.shape[1]
    row_count = lax.axis_size("row")
    contract = (((0,), (0,)), ((), ()))
    factor = -1.0 / math.sqrt(NOCC * NVIR)
    window = ROWS_DEV * row_count
    start_col = lax.axis_index("col") * block_cols
    plane_cols = NB * NC
    per_col = block_cols // plane_cols
    spread = row_count // per_col
    sub_rows = ROWS_DEV // spread

    def spread_planes(waves):
        share = waves.shape[0]
        shaped = waves.reshape(share, per_col, 1, plane_cols)
        shaped = jnp.broadcast_to(shaped, (share, per_col, spread, plane_cols))
        return shaped.reshape(share, row_count * plane_cols)

    def pick_rows(waves):
        share = waves.shape[0]
        shaped = place(waves, window, start_col).reshape(share, row_count, spread, sub_rows)
        shaped = jnp.transpose(shaped, (0, 2, 1, 3))[:, None]
        shaped = jnp.broadcast_to(shaped, (share, per_col, spread, row_count, sub_rows))
        return shaped.reshape(share, row_count * row_count * sub_rows)

    plane_occ, plane_vir = (
        lax.all_to_all(
            spread_planes(occupied_waves), "row", split_axis=1, concat_axis=0, tiled=True
        ),
        lax.all_to_all(
            spread_planes(virtual_waves), "row", split_axis=1, concat_axis=0, tiled=True
        ),
    )
    part_occ, part_vir = (
        lax.all_to_all(pick_rows(occupied_waves), "row", split_axis=1, concat_axis=0, tiled=True),
        lax.all_to_all(pick_rows(virtual_waves), "row", split_axis=1, concat_axis=0, tiled=True),
    )
    occ_rows, vir_rows = (
        lax.psum(part_occ.astype(jnp.float32).astype(jnp.bfloat16), "col").astype(jnp.float32),
        lax.psum(part_vir.astype(jnp.float32).astype(jnp.bfloat16), "col").astype(jnp.float32),
    )
    occ_rows = scale_rows(occ_rows, occupied_decay)
    vir_rows = scale_rows(vir_rows, virtual_decay)
    green_occ = lax.dot_general(plane_occ, occ_rows, contract, preferred_element_type=jnp.float32)
    green_vir = lax.dot_general(plane_vir, vir_rows, contract, preferred_element_type=jnp.float32)
    polar = green_occ * green_vir * factor
    cube = polar.reshape(1, NB, NC, row_count * sub_rows)
    real_part, imag_part = real_step(cube, "abcr,cw->wabr", NC)
    real_part, imag_part = complex_step(real_part, imag_part, "wabr,bv->wavr", NB)
    blocked = (NC, 1, NB, row_count, sub_rows)
    real_part, imag_part = (
        lax.all_to_all(
            lax.all_to_all(
                real_part.reshape(blocked), "row", split_axis=3, concat_axis=3, tiled=True
            ),
            "col",
            split_axis=0,
            concat_axis=1,
            tiled=True,
        ),
        lax.all_to_all(
            lax.all_to_all(
                imag_part.reshape(blocked), "row", split_axis=3, concat_axis=3, tiled=True
            ),
            "col",
            split_axis=0,
            concat_axis=1,
            tiled=True,
        ),
    )

    def settle(part):
        kc_share = part.shape[0]
        part = part.reshape(kc_share, part.shape[1], NB, per_col, spread, sub_rows)
        part = jnp.transpose(part, (0, 1, 3, 2, 4, 5))
        return part.reshape(kc_share, NA, NB, ROWS_DEV)

    real_part, imag_part = complex_step(settle(real_part), settle(imag_part), "wavr,au->rwuv", NA)
    normal = 1.0 / math.sqrt(NGRID)
    final_shape = (real_part.shape[0], real_part.shape[1], NA * NB)
    return ((real_part * normal).reshape(final_shape), (imag_part * normal).reshape(final_shape))


def solution(mesh):
    in_specs = (P("row", "col"), P("row", "col"), P(), P())
    out_specs = (P("row", "col", None), P("row", "col", None))
    return jax.shard_map(
        on_device, mesh=mesh, in_specs=in_specs, out_specs=out_specs, check_vma=False
    )
```

profile of v0, /device:TPU:10, one launch (start us, length us, event | category | flops | bytes accessed | tf_op | source)
XLA Modules:
  0.0 507.3 jit_solution(10017124884010591523)
XLA Ops:
  16.1 12.9 %all-to-all-done.2 = bf16[32,16,512]{2,0,1:T(8,128)(2,1)S(1)} async-done(((bf16[32,16,512]{2,0,1:T(8,128)(2,1)}), bf16[32,16,512]{2,0,1:T(8,128)(2,1)S(1)}, u32[]{:S(2)}, u32[]{:S(2)}) %all-to-all-start.2) | async-done | bytes 524320 | tf_op jit(solution)/shard_map/all_to_all | solution.py:85
  36.8 23.0 %all-to-all-done = bf16[64,16,512]{2,0,1:T(8,128)(2,1)S(1)} async-done(((bf16[64,16,512]{2,0,1:T(8,128)(2,1)}), bf16[64,16,512]{2,0,1:T(8,128)(2,1)S(1)}, u32[]{:S(2)}, u32[]{:S(2)}) %all-to-all-start) | async-done | bytes 1048608 | tf_op jit(solution)/shard_map/all_to_all | solution.py:84
  67.1 46.1 %all-to-all-done.1 = bf16[64,16,1024]{2,0,1:T(8,128)(2,1)S(1)} async-done(((bf16[64,16,1024]{2,0,1:T(8,128)(2,1)}), bf16[64,16,1024]{2,0,1:T(8,128)(2,1)S(1)}, u32[]{:S(2)}, u32[]{:S(2)}) %all-to-all-start.1) | async-done | bytes 2097184 | tf_op jit(solution)/shard_map/all_to_all | solution.py:76
  119.0 55.5 %all-reduce.3.cloned.1.call-done = (bf16[1024,512]{1,0:T(8,128)(2,1)}, bf16[512,512]{1,0:T(8,128)(2,1)}) async-done(((bf16[1024,512]{1,0:T(8,128)(2,1)}, bf16[512,512]{1,0:T(8,128)(2,1)}), (bf16[1024,512]{1,0:T(8,128)(2,1)}, bf16[512,512]{1,0:T(8,128)(2,1)})) %all-reduce.3.cloned.1.call-update) | async-done | bytes 1572880 | tf_op jit(solution)/shard_map/psum | solution.py:88
  205.8 9.3 %copy.71 = f32[32,1,32,16,32]{4,2,0,1,3:T(8,128)} copy(f32[32,1,32,16,32]{4,3,2,0,1:T(8,128)} %reshape.86) | data formatting | bytes 4194304 | tf_op jit(solution)/shard_map/reshape | solution.py:112
  215.1 8.6 %reshape.99 = f32[16,1,32768]{2,1,0:T(1,128)} reshape(f32[16,1,32,32,32]{4,3,2,1,0:T(8,128)} %bitcast.113) | data formatting | bytes 4194304
  244.9 9.3 %copy.72 = f32[32,1,32,16,32]{4,2,0,1,3:T(8,128)} copy(f32[32,1,32,16,32]{4,3,2,0,1:T(8,128)} %reshape.83) | data formatting | bytes 4194304 | tf_op jit(solution)/shard_map/reshape | solution.py:103
  254.2 8.6 %reshape.95 = f32[16,1,32768]{2,1,0:T(1,128)} reshape(f32[16,1,32,32,32]{4,3,2,1,0:T(8,128)} %bitcast.114) | data formatting | bytes 4194304
  262.7 14.2 %all-to-all-done.6 = f32[16,1,32768]{2,1,0:T(1,128)} async-done(((f32[16,1,32768]{2,1,0:T(1,128)}), f32[16,1,32768]{2,1,0:T(1,128)}, u32[]{:S(2)}, u32[]{:S(2)}) %all-to-all-start.6) | async-done | bytes 2097184 | tf_op jit(solution)/shard_map/all_to_all | solution.py:111
  295.4 14.2 %copy.45 = f32[32,1,32,16,32]{4,3,2,1,0:T(8,128)} copy(f32[32,1,32,16,32]{4,2,0,1,3:T(8,128)} %bitcast.115) | data formatting | bytes 4194304 | tf_op jit(solution)/shard_map/all_to_all | solution.py:111
  316.4 13.3 %all-to-all-done.4 = f32[16,1,32768]{2,1,0:T(1,128)} async-done(((f32[16,1,32768]{2,1,0:T(1,128)}), f32[16,1,32768]{2,1,0:T(1,128)}, u32[]{:S(2)}, u32[]{:S(2)}) %all-to-all-start.4) | async-done | bytes 2097184 | tf_op jit(solution)/shard_map/all_to_all | solution.py:102
  334.7 7.3 %reduce = f32[16,32768]{1,0:T(8,128)S(1)} reduce(f32[16,1,32768]{2,1,0:T(1,128)} %all-to-all-done.4, f32[]{:T(128)} %broadcast.102), dimensions={1}, to_apply=%all_to_all.94.reduce_sub_computation | reduce | bytes 4194308 | tf_op jit(solution)/shard_map/all_to_all | solution.py:102
  346.7 14.2 %copy.40 = f32[32,1,32,16,32]{4,3,2,1,0:T(8,128)} copy(f32[32,1,32,16,32]{4,2,0,1,3:T(8,128)} %bitcast.116) | data formatting | bytes 4194304 | tf_op jit(solution)/shard_map/all_to_all | solution.py:102
  372.6 8.5 %reduce.3 = f32[2,262144]{1,0:T(2,128)S(1)} reduce(f32[2,1,262144]{2,1,0:T(1,128)} %all-to-all-done.7, f32[]{:T(128)} %broadcast.102), dimensions={1}, to_apply=%all_to_all.99.reduce_sub_computation | reduce | bytes 4194308 | tf_op jit(solution)/shard_map/all_to_all | solution.py:110
  387.5 7.7 %copy.46 = f32[2,16,1,32,16,32]{5,4,0,3,1,2:T(8,128)} copy(f32[2,16,1,32,16,32]{5,4,3,1,0,2:T(8,128)} %bitcast.117) | data formatting | bytes 4194304 | tf_op jit(solution)/shard_map/all_to_all | solution.py:110
  398.3 8.2 %reduce.1 = f32[2,262144]{1,0:T(2,128)S(1)} reduce(f32[2,1,262144]{2,1,0:T(1,128)} %all-to-all-done.5, f32[]{:T(128)} %broadcast.102), dimensions={1}, to_apply=%all_to_all.95.reduce_sub_computation | reduce | bytes 4194308 | tf_op jit(solution)/shard_map/all_to_all | solution.py:101
  417.6 9.5 %fusion.22 = f32[32,16,32,32]{3,0,2,1:T(8,128)} fusion(f32[16,32,32,32]{3,1,2,0:T(8,128)S(1)} %bitcast.111), kind=kOutput, calls=%fused_computation.31 | convolution fusion | flops 201340928 | bytes 4194304 | tf_op jit(solution)/shard_map/wavr,au->rwuv/dot_general | solution.py:24
  427.1 9.8 %fusion.20 = f32[32,16,32,32]{3,0,2,1:T(8,128)} fusion(f32[16,32,32,32]{3,1,2,0:T(8,128)S(1)} %bitcast.109), kind=kOutput, calls=%fused_computation.29 | convolution fusion | flops 201340928 | bytes 4194304 | tf_op jit(solution)/shard_map/wavr,au->rwuv/dot_general | solution.py:24
  436.9 12.1 %multiply_bitcast_fusion.1 = f32[32,16,32,32]{0,2,3,1:T(8,128)} fusion(f32[32,16,32,32]{3,0,2,1:T(8,128)} %fusion.22, f32[16,32,32,32]{3,1,2,0:T(8,128)S(1)} %bitcast.110), kind=kOutput, calls=%fused_computation.1 | convolution fusion | flops 202389504 | bytes 6291456 | tf_op jit(solution)/shard_map/wavr,au->rwuv/dot_general | solution.py:24
  449.0 12.4 %multiply_bitcast_fusion = f32[32,16,32,32]{0,2,3,1:T(8,128)} fusion(f32[32,16,32,32]{3,0,2,1:T(8,128)} %fusion.20, f32[16,32,32,32]{3,1,2,0:T(8,128)S(1)} %bitcast.112), kind=kOutput, calls=%fused_computation | convolution fusion | flops 202389504 | bytes 6291456 | tf_op jit(solution)/shard_map/wavr,au->rwuv/dot_general | solution.py:24
  461.4 11.7 %copy.48 = f32[32,16,32,32]{3,2,1,0:T(8,128)} copy(f32[32,16,32,32]{0,2,3,1:T(8,128)} %multiply_bitcast_fusion) | data formatting | bytes 4194304 | tf_op jit(solution)/shard_map/mul | solution.py:130
  473.1 7.7 %reshape.90 = f32[32,16,1024]{2,1,0:T(8,128)} reshape(f32[32,16,32,32]{3,2,1,0:T(8,128)} %copy.48) | data formatting | bytes 4194304 | tf_op jit(solution)/shard_map/reshape | solution.py:130
  480.8 11.7 %copy.47 = f32[32,16,32,32]{3,2,1,0:T(8,128)} copy(f32[32,16,32,32]{0,2,3,1:T(8,128)} %multiply_bitcast_fusion.1) | data formatting | bytes 4194304 | tf_op jit(solution)/shard_map/mul | solution.py:130
  492.5 7.7 %reshape.89 = f32[32,16,1024]{2,1,0:T(8,128)} reshape(f32[32,16,32,32]{3,2,1,0:T(8,128)} %copy.47) | data formatting | bytes 4194304 | tf_op jit(solution)/shard_map/reshape | solution.py:130
  (64 shorter events, 149.4 us)
Async XLA Ops:
  8.6 7.3 %copy-start.2 = (bf16[64,16384]{1,0:T(8,128)(2,1)S(1)}, bf16[64,16384]{1,0:T(8,128)(2,1)}, u32[]{:S(2)}) copy-start(bf16[64,16384]{1,0:T(8,128)(2,1)} %param.4) | copy-start | bytes 6291460
  9.4 19.5 %all-to-all-start.2 = ((bf16[32,16,512]{2,0,1:T(8,128)(2,1)}), bf16[32,16,512]{2,0,1:T(8,128)(2,1)S(1)}, u32[]{:S(2)}, u32[]{:S(2)}) async-start(bf16[32,16,512]{2,0,1:T(8,128)(2,1)} %broadcast_in_dim.11), calls=%async_computation.2 | async-start | bytes 1048576 | tf_op jit(solution)/shard_map/all_to_all | solution.py:85
  29.0 1.1 copy-start.5
  30.1 29.7 %all-to-all-start = ((bf16[64,16,512]{2,0,1:T(8,128)(2,1)}), bf16[64,16,512]{2,0,1:T(8,128)(2,1)S(1)}, u32[]{:S(2)}, u32[]{:S(2)}) async-start(bf16[64,16,512]{2,0,1:T(8,128)(2,1)} %broadcast_in_dim.9), calls=%async_computation | async-start | bytes 2097152 | tf_op jit(solution)/shard_map/all_to_all | solution.py:84
  59.9 1.0 copy-start.4
  60.8 5.2 %copy-start.3 = (bf16[32,16384]{1,0:T(8,128)(2,1)S(1)}, bf16[32,16384]{1,0:T(8,128)(2,1)}, u32[]{:S(2)}) copy-start(bf16[32,16384]{1,0:T(8,128)(2,1)} %param.5) | copy-start | bytes 3145732
  60.8 52.4 %all-to-all-start.1 = ((bf16[64,16,1024]{2,0,1:T(8,128)(2,1)}), bf16[64,16,1024]{2,0,1:T(8,128)(2,1)S(1)}, u32[]{:S(2)}, u32[]{:S(2)}) async-start(bf16[64,16,1024]{2,0,1:T(8,128)(2,1)} %bitcast.123), calls=%async_computation.1 | async-start | bytes 4194304 | tf_op jit(solution)/shard_map/all_to_all | solution.py:76
  67.1 107.4 %copy-start.6 = (f32[1024]{0:T(1024)S(1)}, f32[1024]{0:T(1024)}, u32[]{:S(2)}) copy-start(f32[1024]{0:T(1024)} %param.6) | copy-start | bytes 12292
  113.2 65.3 %all-to-all-start.3 = ((bf16[32,16,1024]{2,0,1:T(8,128)(2,1)}), bf16[32,16,1024]{2,0,1:T(8,128)(2,1)S(1)}, u32[]{:S(2)}, u32[]{:S(2)}) async-start(bf16[32,16,1024]{2,0,1:T(8,128)(2,1)} %bitcast.126), calls=%async_computation.3 | async-start | bytes 2097152 | tf_op jit(solution)/shard_map/all_to_all | solution.py:79
  118.3 56.3 %all-reduce.3.cloned.1.call-start = ((), (), s32[]{:S(2)}) async-start(), calls=%async_computation.8 | async-start | bytes 3145728 | tf_op jit(solution)/shard_map/psum | solution.py:88
  174.5 3.9 copy-start.7
  184.5 1.3 copy-start.1
  187.7 4.3 copy-start
  223.7 53.3 %all-to-all-start.6 = ((f32[16,1,32768]{2,1,0:T(1,128)}), f32[16,1,32768]{2,1,0:T(1,128)}, u32[]{:S(2)}, u32[]{:S(2)}) async-start(f32[16,1,32768]{2,1,0:T(1,128)} %reshape.99), calls=%async_computation.6 | async-start | bytes 4194304 | tf_op jit(solution)/shard_map/all_to_all | solution.py:111
  277.0 52.7 %all-to-all-start.4 = ((f32[16,1,32768]{2,1,0:T(1,128)}), f32[16,1,32768]{2,1,0:T(1,128)}, u32[]{:S(2)}, u32[]{:S(2)}) async-start(f32[16,1,32768]{2,1,0:T(1,128)} %reshape.95), calls=%async_computation.4 | async-start | bytes 4194304 | tf_op jit(solution)/shard_map/all_to_all | solution.py:102
  329.7 38.1 %all-to-all-start.7 = ((f32[2,1,262144]{2,1,0:T(1,128)}), f32[2,1,262144]{2,1,0:T(1,128)}, u32[]{:S(2)}, u32[]{:S(2)}) async-start(f32[2,1,262144]{2,1,0:T(1,128)} %reshape.101), calls=%async_computation.7 | async-start | bytes 4194304 | tf_op jit(solution)/shard_map/all_to_all | solution.py:110
  367.8 30.6 %all-to-all-start.5 = ((f32[2,1,262144]{2,1,0:T(1,128)}), f32[2,1,262144]{2,1,0:T(1,128)}, u32[]{:S(2)}, u32[]{:S(2)}) async-start(f32[2,1,262144]{2,1,0:T(1,128)} %reshape.97), calls=%async_computation.5 | async-start | bytes 4194304 | tf_op jit(solution)/shard_map/all_to_all | solution.py:101
  413.0 14.1 %slice-start = ((s8[8388608]{0:T(1024)(128)(4,1)}), s8[4194304]{0:T(1024)(128)(4,1)S(1)}, s32[]{:S(2)}) async-start(s8[8388608]{0:T(1024)(128)(4,1)} %bitcast.107), calls=%async_computation.9 | async-start | bytes 8388608
  417.6 9.5 %slice-start.1 = ((s8[8388608]{0:T(1024)(128)(4,1)}), s8[4194304]{0:T(1024)(128)(4,1)S(1)}, s32[]{:S(2)}) async-start(s8[8388608]{0:T(1024)(128)(4,1)} %bitcast.107), calls=%async_computation.10 | async-start | bytes 8388608
Sparse Core Ops, SparseCore 0:
  122.0 52.4 all-reduce.2
where the time goes:
time: 513 us; the launch traced here: 507 us
  local copies, waits for them, and re-layouts  175 us (34%)
  waiting for transfers between devices  169 us (33%)
  matrix products  74.2 us (14%)
  starting transfers between devices  43.2 us (8%)
  other arithmetic  31.2 us (6%)
  between operations  14.5 us (3%)
    dot_general x10, matrix products, apply_table(): return jnp.einsum(form, data, table, precision=lax.Precision.HIGHEST)  66.3 us
    unnamed x28, local copies, waits for them, and re-layouts  55.6 us
    psum x1, waiting for transfers between devices, on_device(): lax.psum(part_occ.astype(jnp.float32).astype(jnp.bfloat16), 'col')  55.5 us
    all_to_all x1, waiting for transfers between devices, on_device(): lax.all_to_all(spread_planes(occupied_waves), 'row', split_axis=1, concat...  46.1 us
    all_to_all x1, waiting for transfers between devices, on_device(): lax.all_to_all(pick_rows(occupied_waves), 'row', split_axis=1, concat_axi...  23 us
    reshape x2, local copies, waits for them, and re-layouts, on_device(): imag_part.reshape(blocked)  15.7 us
    reshape x2, local copies, waits for them, and re-layouts, on_device(): real_part.reshape(blocked)  15.5 us
    all_to_all x2, local copies, waits for them, and re-layouts, on_device(): lax.all_to_all(real_part.reshape(blocked), 'row', split_axis=3, concat_ax...  14.8 us
  transfers between devices with their start and end apart: 9, of which 7 were waited for; matrix products, arithmetic and copies ran while one was open for 26% of the time, Pallas kernels for 0%

commit v1 on v0

--- a/solution.py
+++ b/solution.py
@@ -85,7 +85,9 @@
         lax.all_to_all(pick_rows(virtual_waves), "row", split_axis=1, concat_axis=0, tiled=True),
     )
     occ_rows, vir_rows = (
-        lax.psum(part_occ.astype(jnp.float32).astype(jnp.bfloat16), "col").astype(jnp.float32),
+        jnp.sum(
+            lax.all_gather(part_occ.astype(jnp.float32).astype(jnp.bfloat16), "col"), axis=0
+        ).astype(jnp.float32),
         lax.psum(part_vir.astype(jnp.float32).astype(jnp.bfloat16), "col").astype(jnp.float32),
     )
     occ_rows = scale_rows(occ_rows, occupied_decay)

time: 513 us -> 487 us (0.949)
  waiting for transfers between devices: 169 us -> 140 us
    psum x1, waiting for transfers between devices: 55.5 us -> 26.6 us  [on_device(): lax.psum(part_vir.astype(jnp.float32).astype(jnp.bfloat16), 'col')]
  transfers between devices with their start and end apart: 9 -> 10, of which waited for: 7 -> 7; matrix products, arithmetic and copies ran while one was open for 26% -> 27% of each run, Pallas kernels for 0% -> 0%
where the time goes in v1:
time: 487 us; the launch traced here: 481 us
  local copies, waits for them, and re-layouts  175 us (36%)
  waiting for transfers between devices  140 us (29%)
  matrix products  73.3 us (15%)
  starting transfers between devices  43.2 us (9%)
  other arithmetic  33.5 us (7%)
  between operations  14.8 us (3%)
    dot_general x10, matrix products, apply_table(): return jnp.einsum(form, data, table, precision=lax.Precision.HIGHEST)  66.4 us
    unnamed x28, local copies, waits for them, and re-layouts  55.7 us
    all_to_all x1, waiting for transfers between devices, on_device(): lax.all_to_all(spread_planes(occupied_waves), 'row', split_axis=1, concat...  45.3 us
    psum x1, waiting for transfers between devices, on_device(): lax.psum(part_vir.astype(jnp.float32).astype(jnp.bfloat16), 'col')  26.6 us
    all_to_all x1, waiting for transfers between devices, on_device(): lax.all_to_all(pick_rows(occupied_waves), 'row', split_axis=1, concat_axi...  23 us
    reshape x2, local copies, waits for them, and re-layouts, on_device(): imag_part.reshape(blocked)  15.9 us
    reshape x2, local copies, waits for them, and re-layouts, on_device(): real_part.reshape(blocked)  15.5 us
    all_to_all x2, local copies, waits for them, and re-layouts, on_device(): lax.all_to_all(real_part.reshape(blocked), 'row', split_axis=3, concat_ax...  14.7 us
  transfers between devices with their start and end apart: 10, of which 7 were waited for; matrix products, arithmetic and copies ran while one was open for 27% of the time, Pallas kernels for 0%

profile of v1, /device:TPU:10, one launch (start us, length us, event | category | flops | bytes accessed | tf_op | source)
XLA Modules:
  0.0 480.5 jit_solution(6654739943282514132)
XLA Ops:
  16.1 12.9 %all-to-all-done.2 = bf16[32,16,512]{2,0,1:T(8,128)(2,1)S(1)} async-done(((bf16[32,16,512]{2,0,1:T(8,128)(2,1)}), bf16[32,16,512]{2,0,1:T(8,128)(2,1)S(1)}, u32[]{:S(2)}, u32[]{:S(2)}) %all-to-all-start.2) | async-done | bytes 524320 | tf_op jit(solution)/shard_map/all_to_all | solution.py:85
  36.8 23.0 %all-to-all-done = bf16[64,16,512]{2,0,1:T(8,128)(2,1)S(1)} async-done(((bf16[64,16,512]{2,0,1:T(8,128)(2,1)}), bf16[64,16,512]{2,0,1:T(8,128)(2,1)S(1)}, u32[]{:S(2)}, u32[]{:S(2)}) %all-to-all-start) | async-done | bytes 1048608 | tf_op jit(solution)/shard_map/all_to_all | solution.py:84
  67.9 45.3 %all-to-all-done.1 = bf16[64,16,1024]{2,0,1:T(8,128)(2,1)S(1)} async-done(((bf16[64,16,1024]{2,0,1:T(8,128)(2,1)}), bf16[64,16,1024]{2,0,1:T(8,128)(2,1)S(1)}, u32[]{:S(2)}, u32[]{:S(2)}) %all-to-all-start.1) | async-done | bytes 2097184 | tf_op jit(solution)/shard_map/all_to_all | solution.py:76
  124.4 26.6 %all-reduce.2.cloned.1.call-done = bf16[512,512]{1,0:T(8,128)(2,1)} async-done(((bf16[512,512]{1,0:T(8,128)(2,1)}), bf16[512,512]{1,0:T(8,128)(2,1)}) %all-reduce.2.cloned.1.call-update) | async-done | bytes 524304 | tf_op jit(solution)/shard_map/psum | solution.py:91
  178.9 9.3 %copy.71 = f32[32,1,32,16,32]{4,2,0,1,3:T(8,128)} copy(f32[32,1,32,16,32]{4,3,2,0,1:T(8,128)} %reshape.87) | data formatting | bytes 4194304 | tf_op jit(solution)/shard_map/reshape | solution.py:114
  188.2 8.6 %reshape.100 = f32[16,1,32768]{2,1,0:T(1,128)} reshape(f32[16,1,32,32,32]{4,3,2,1,0:T(8,128)} %bitcast.113) | data formatting | bytes 4194304
  217.9 9.3 %copy.72 = f32[32,1,32,16,32]{4,2,0,1,3:T(8,128)} copy(f32[32,1,32,16,32]{4,3,2,0,1:T(8,128)} %reshape.84) | data formatting | bytes 4194304 | tf_op jit(solution)/shard_map/reshape | solution.py:105
  227.2 8.6 %reshape.96 = f32[16,1,32768]{2,1,0:T(1,128)} reshape(f32[16,1,32,32,32]{4,3,2,1,0:T(8,128)} %bitcast.114) | data formatting | bytes 4194304
  235.8 14.2 %all-to-all-done.6 = f32[16,1,32768]{2,1,0:T(1,128)} async-done(((f32[16,1,32768]{2,1,0:T(1,128)}), f32[16,1,32768]{2,1,0:T(1,128)}, u32[]{:S(2)}, u32[]{:S(2)}) %all-to-all-start.6) | async-done | bytes 2097184 | tf_op jit(solution)/shard_map/all_to_all | solution.py:113
  268.1 14.2 %copy.45 = f32[32,1,32,16,32]{4,3,2,1,0:T(8,128)} copy(f32[32,1,32,16,32]{4,2,0,1,3:T(8,128)} %bitcast.115) | data formatting | bytes 4194304 | tf_op jit(solution)/shard_map/all_to_all | solution.py:113
  289.2 13.4 %all-to-all-done.4 = f32[16,1,32768]{2,1,0:T(1,128)} async-done(((f32[16,1,32768]{2,1,0:T(1,128)}), f32[16,1,32768]{2,1,0:T(1,128)}, u32[]{:S(2)}, u32[]{:S(2)}) %all-to-all-start.4) | async-done | bytes 2097184 | tf_op jit(solution)/shard_map/all_to_all | solution.py:104
  307.7 7.2 %reduce.1 = f32[16,32768]{1,0:T(8,128)S(1)} reduce(f32[16,1,32768]{2,1,0:T(1,128)} %all-to-all-done.4, f32[]{:T(128)} %broadcast.102), dimensions={1}, to_apply=%all_to_all.91.reduce_sub_computation | reduce | bytes 4194308 | tf_op jit(solution)/shard_map/all_to_all | solution.py:104
  319.7 14.2 %copy.40 = f32[32,1,32,16,32]{4,3,2,1,0:T(8,128)} copy(f32[32,1,32,16,32]{4,2,0,1,3:T(8,128)} %bitcast.116) | data formatting | bytes 4194304 | tf_op jit(solution)/shard_map/all_to_all | solution.py:104
  345.6 8.2 %reduce.4 = f32[2,262144]{1,0:T(2,128)S(1)} reduce(f32[2,1,262144]{2,1,0:T(1,128)} %all-to-all-done.7, f32[]{:T(128)} %broadcast.102), dimensions={1}, to_apply=%all_to_all.96.reduce_sub_computation | reduce | bytes 4194308 | tf_op jit(solution)/shard_map/all_to_all | solution.py:112
  360.2 7.7 %copy.46 = f32[2,16,1,32,16,32]{5,4,0,3,1,2:T(8,128)} copy(f32[2,16,1,32,16,32]{5,4,3,1,0,2:T(8,128)} %bitcast.117) | data formatting | bytes 4194304 | tf_op jit(solution)/shard_map/all_to_all | solution.py:112
  371.3 8.2 %reduce.2 = f32[2,262144]{1,0:T(2,128)S(1)} reduce(f32[2,1,262144]{2,1,0:T(1,128)} %all-to-all-done.5, f32[]{:T(128)} %broadcast.102), dimensions={1}, to_apply=%all_to_all.92.reduce_sub_computation | reduce | bytes 4194308 | tf_op jit(solution)/shard_map/all_to_all | solution.py:103
  390.6 9.5 %fusion.22 = f32[32,16,32,32]{3,0,2,1:T(8,128)} fusion(f32[16,32,32,32]{3,1,2,0:T(8,128)S(1)} %bitcast.111), kind=kOutput, calls=%fused_computation.31 | convolution fusion | flops 201340928 | bytes 4194304 | tf_op jit(solution)/shard_map/wavr,au->rwuv/dot_general | solution.py:24
  400.1 9.8 %fusion.20 = f32[32,16,32,32]{3,0,2,1:T(8,128)} fusion(f32[16,32,32,32]{3,1,2,0:T(8,128)S(1)} %bitcast.109), kind=kOutput, calls=%fused_computation.29 | convolution fusion | flops 201340928 | bytes 4194304 | tf_op jit(solution)/shard_map/wavr,au->rwuv/dot_general | solution.py:24
  409.9 12.1 %multiply_bitcast_fusion.1 = f32[32,16,32,32]{0,2,3,1:T(8,128)} fusion(f32[32,16,32,32]{3,0,2,1:T(8,128)} %fusion.22, f32[16,32,32,32]{3,1,2,0:T(8,128)S(1)} %bitcast.110), kind=kOutput, calls=%fused_computation.1 | convolution fusion | flops 202389504 | bytes 6291456 | tf_op jit(solution)/shard_map/wavr,au->rwuv/dot_general | solution.py:24
  422.0 12.4 %multiply_bitcast_fusion = f32[32,16,32,32]{0,2,3,1:T(8,128)} fusion(f32[32,16,32,32]{3,0,2,1:T(8,128)} %fusion.20, f32[16,32,32,32]{3,1,2,0:T(8,128)S(1)} %bitcast.112), kind=kOutput, calls=%fused_computation | convolution fusion | flops 202389504 | bytes 6291456 | tf_op jit(solution)/shard_map/wavr,au->rwuv/dot_general | solution.py:24
  434.5 11.6 %copy.48 = f32[32,16,32,32]{3,2,1,0:T(8,128)} copy(f32[32,16,32,32]{0,2,3,1:T(8,128)} %multiply_bitcast_fusion) | data formatting | bytes 4194304 | tf_op jit(solution)/shard_map/mul | solution.py:132
  446.1 7.7 %reshape.91 = f32[32,16,1024]{2,1,0:T(8,128)} reshape(f32[32,16,32,32]{3,2,1,0:T(8,128)} %copy.48) | data formatting | bytes 4194304 | tf_op jit(solution)/shard_map/reshape | solution.py:132
  453.8 11.6 %copy.47 = f32[32,16,32,32]{3,2,1,0:T(8,128)} copy(f32[32,16,32,32]{0,2,3,1:T(8,128)} %multiply_bitcast_fusion.1) | data formatting | bytes 4194304 | tf_op jit(solution)/shard_map/mul | solution.py:132
  465.5 7.7 %reshape.90 = f32[32,16,1024]{2,1,0:T(8,128)} reshape(f32[32,16,32,32]{3,2,1,0:T(8,128)} %copy.47) | data formatting | bytes 4194304 | tf_op jit(solution)/shard_map/reshape | solution.py:132
  (68 shorter events, 152.2 us)
Async XLA Ops:
  8.6 7.3 %copy-start.2 = (bf16[64,16384]{1,0:T(8,128)(2,1)S(1)}, bf16[64,16384]{1,0:T(8,128)(2,1)}, u32[]{:S(2)}) copy-start(bf16[64,16384]{1,0:T(8,128)(2,1)} %param.4) | copy-start | bytes 6291460
  9.4 19.5 %all-to-all-start.2 = ((bf16[32,16,512]{2,0,1:T(8,128)(2,1)}), bf16[32,16,512]{2,0,1:T(8,128)(2,1)S(1)}, u32[]{:S(2)}, u32[]{:S(2)}) async-start(bf16[32,16,512]{2,0,1:T(8,128)(2,1)} %broadcast_in_dim.11), calls=%async_computation.2 | async-start | bytes 1048576 | tf_op jit(solution)/shard_map/all_to_all | solution.py:85
  29.0 1.1 copy-start.5
  30.1 29.7 %all-to-all-start = ((bf16[64,16,512]{2,0,1:T(8,128)(2,1)}), bf16[64,16,512]{2,0,1:T(8,128)(2,1)S(1)}, u32[]{:S(2)}, u32[]{:S(2)}) async-start(bf16[64,16,512]{2,0,1:T(8,128)(2,1)} %broadcast_in_dim.9), calls=%async_computation | async-start | bytes 2097152 | tf_op jit(solution)/shard_map/all_to_all | solution.py:84
  59.9 1.0 copy-start.4
  60.8 6.0 %copy-start.3 = (bf16[32,16384]{1,0:T(8,128)(2,1)S(1)}, bf16[32,16384]{1,0:T(8,128)(2,1)}, u32[]{:S(2)}) copy-start(bf16[32,16384]{1,0:T(8,128)(2,1)} %param.5) | copy-start | bytes 3145732
  60.8 52.4 %all-to-all-start.1 = ((bf16[64,16,1024]{2,0,1:T(8,128)(2,1)}), bf16[64,16,1024]{2,0,1:T(8,128)(2,1)S(1)}, u32[]{:S(2)}, u32[]{:S(2)}) async-start(bf16[64,16,1024]{2,0,1:T(8,128)(2,1)} %bitcast.123), calls=%async_computation.1 | async-start | bytes 4194304 | tf_op jit(solution)/shard_map/all_to_all | solution.py:76
  66.1 53.0 %all-gather.2.cloned.1.call-start = ((), (), s32[]{:S(2)}) async-start(), calls=%async_computation.8 | async-start | bytes 3145728 | tf_op jit(solution)/shard_map/all_gather | solution.py:89
  113.2 37.8 %all-to-all-start.3 = ((bf16[32,16,1024]{2,0,1:T(8,128)(2,1)}), bf16[32,16,1024]{2,0,1:T(8,128)(2,1)}, u32[]{:S(2)}, u32[]{:S(2)}) async-start(bf16[32,16,1024]{2,0,1:T(8,128)(2,1)} %bitcast.126), calls=%async_computation.3 | async-start | bytes 2097152 | tf_op jit(solution)/shard_map/all_to_all | solution.py:79
  118.3 3.4 copy-start.6
  118.3 32.7 %all-reduce.2.cloned.1.call-start = ((), (), s32[]{:S(2)}) async-start(), calls=%async_computation.9 | async-start | bytes 1048576 | tf_op jit(solution)/shard_map/psum | solution.py:91
  121.7 29.3 %copy-start.7 = (f32[512]{0:T(512)S(1)}, f32[512]{0:T(512)}, u32[]{:S(2)}) copy-start(f32[512]{0:T(512)} %param.7) | copy-start | bytes 6148
  157.3 1.3 copy-start.1
  160.6 4.3 copy-start
  196.7 53.3 %all-to-all-start.6 = ((f32[16,1,32768]{2,1,0:T(1,128)}), f32[16,1,32768]{2,1,0:T(1,128)}, u32[]{:S(2)}, u32[]{:S(2)}) async-start(f32[16,1,32768]{2,1,0:T(1,128)} %reshape.100), calls=%async_computation.6 | async-start | bytes 4194304 | tf_op jit(solution)/shard_map/all_to_all | solution.py:113
  250.0 52.5 %all-to-all-start.4 = ((f32[16,1,32768]{2,1,0:T(1,128)}), f32[16,1,32768]{2,1,0:T(1,128)}, u32[]{:S(2)}, u32[]{:S(2)}) async-start(f32[16,1,32768]{2,1,0:T(1,128)} %reshape.96), calls=%async_computation.4 | async-start | bytes 4194304 | tf_op jit(solution)/shard_map/all_to_all | solution.py:104
  302.5 38.2 %all-to-all-start.7 = ((f32[2,1,262144]{2,1,0:T(1,128)}), f32[2,1,262144]{2,1,0:T(1,128)}, u32[]{:S(2)}, u32[]{:S(2)}) async-start(f32[2,1,262144]{2,1,0:T(1,128)} %reshape.102), calls=%async_computation.7 | async-start | bytes 4194304 | tf_op jit(solution)/shard_map/all_to_all | solution.py:112
  340.7 30.6 %all-to-all-start.5 = ((f32[2,1,262144]{2,1,0:T(1,128)}), f32[2,1,262144]{2,1,0:T(1,128)}, u32[]{:S(2)}, u32[]{:S(2)}) async-start(f32[2,1,262144]{2,1,0:T(1,128)} %reshape.98), calls=%async_computation.5 | async-start | bytes 4194304 | tf_op jit(solution)/shard_map/all_to_all | solution.py:103
  386.0 14.1 %slice-start = ((s8[8388608]{0:T(1024)(128)(4,1)}), s8[4194304]{0:T(1024)(128)(4,1)S(1)}, s32[]{:S(2)}) async-start(s8[8388608]{0:T(1024)(128)(4,1)} %bitcast.107), calls=%async_computation.10 | async-start | bytes 8388608
  390.6 9.5 %slice-start.1 = ((s8[8388608]{0:T(1024)(128)(4,1)}), s8[4194304]{0:T(1024)(128)(4,1)S(1)}, s32[]{:S(2)}) async-start(s8[8388608]{0:T(1024)(128)(4,1)} %bitcast.107), calls=%async_computation.11 | async-start | bytes 8388608
Sparse Core Ops, SparseCore 0:
  69.0 33.9 all-gather.1
  121.4 29.5 all-reduce.1
